TPU v7x, 256 devices: a whole 4x4x8 slice. The times are simulated.
256 devices in a mesh: dp: 4 (over x), expert: 64 (over z, y, core).
Axes of the slice: x: 4, y: 4, z: 8, core: 2. Of those that a mesh axis runs over, the one named last changes fastest.
Arguments:
- tokens: bfloat16 [32768, 2048], P(('dp', 'expert')), may hold values from -6 to 6
- expert_ids: int32 [32768, 2], P(('dp', 'expert')), may hold values from 0 to 63, all different within a row; in each aligned block of 128 rows (0 to 127, 128 to 255, ...) at most 5 rows name the same one
- gate_units: int32 [32768, 2], P(('dp', 'expert')), may hold values from 64 to 1023
- capacity: int32 [64], replicated, may hold values from 512 to 1535
- w_gate: bfloat16 [64, 2048, 1408], P('expert', None, 'dp'), may hold values from -0.125 to 0.125
- w_up: bfloat16 [64, 2048, 1408], P('expert', None, 'dp'), may hold values from -0.125 to 0.125
- w_down: bfloat16 [64, 2048, 1408], P('expert', None, 'dp'), may hold values from -0.15625 to 0.15625
Outputs:
- mixed: bfloat16 [32768, 2048], P(('dp', 'expert'))
Inputs may be any that keep to these rules, and one draw needn't show every extreme that they name: `expert_ids`: each row names two different experts; of one device's 128 rows (aligned blocks) no expert is named more than 5 times.
All inputs are finite; a program needn't handle non-finite values.
Results may differ from a plain program's by a relative error of at most 0.0057.
Values may be sent and summed in bfloat16 or wider, within the bound.
A program may use at most 128 MiB of HBM per device.

v0:
```python
import jax
import jax.numpy as jnp
from jax import lax
from jax.sharding import Mesh
from jax.sharding import PartitionSpec as P

DP_EXPERT = ("dp", "expert_0", "expert_1", "expert_2")
EXPERT = ("expert_0", "expert_1", "expert_2")


def neutral_like(shard, identity):
    return jnp.zeros_like(shard) + jnp.asarray(identity, shard.dtype)


def carried_in(shard, axes, combine, identity):
    before = start = neutral_like(shard, identity)
    total = shard
    for axis in reversed(axes):
        length, here = (lax.axis_size(axis), lax.axis_index(axis))
        pieces = lax.all_gather(total, axis)
        inside, total = (start, start)
        for k in range(length):
            passed = k < here
            total = combine(total, pieces[k])
            inside = jnp.where(passed, total, inside)
        before = combine(inside, before)
    return before


def gather_turned(arrays, axis, dims):
    turned = [jnp.moveaxis(a, dim, 0) for a, dim in zip(arrays, dims)]
    both = jnp.concatenate([t.reshape(len(t), -1) for t in turned], axis=1)
    filled, at, finished = (lax.all_gather(both, axis, axis=0, tiled=True), 0, [])
    for t, dim in zip(turned, dims):
        piece = filled[:, at : at + t[0].size].reshape(-1, *t.shape[1:])
        finished.append(jnp.moveaxis(piece, 0, dim))
        at += t[0].size
    return tuple(finished)


def expert_rows(rows, gate_w, up_w, down_w):
    gate = jnp.dot(rows, gate_w, preferred_element_type=jnp.float32)
    up = jnp.dot(rows, up_w, preferred_element_type=jnp.float32)
    hidden = (jax.nn.silu(gate) * up).astype(jnp.bfloat16)
    return lax.dot_general(
        hidden, down_w, (((1,), (1,)), ((), ())), preferred_element_type=jnp.float32
    )


def add_counts(earlier, later):
    return earlier + later


def local(tokens, expert_ids, gate_units, capacity, w_gate, w_up, w_down):
    tok_rows = tokens.shape[0]
    width = tokens.shape[1]
    n_experts = capacity.shape[0]
    most = max(2, 5 * tok_rows // (2 * n_experts))
    slots_all = n_experts * most
    flat = expert_ids.reshape(-1)
    onehot = (flat[:, None] == jnp.arange(n_experts, dtype=jnp.int32)[None, :]).astype(jnp.int32)
    local_rank = jnp.sum((jnp.cumsum(onehot, axis=0) - onehot) * onehot, axis=1)
    counts = jnp.sum(onehot, axis=0)
    offsets = carried_in(counts, DP_EXPERT, add_counts, jnp.zeros_like(counts))
    global_slot = jnp.sum(onehot * offsets[None, :], axis=1) + local_rank
    limit = jnp.sum(onehot * capacity[None, :], axis=1)
    kept = global_slot < limit
    weight = jnp.where(kept, gate_units.reshape(-1).astype(jnp.float32) / 1024.0, jnp.float32(0.0))
    send_slot = flat * most + local_rank
    chosen = (send_slot[None, :] == jnp.arange(slots_all, dtype=jnp.int32)[:, None]) & kept[None, :]
    placing = jnp.sum(chosen.reshape(slots_all, tok_rows, 2).astype(jnp.int32), axis=2).astype(
        jnp.bfloat16
    )
    outgoing = jnp.dot(placing, tokens, preferred_element_type=jnp.float32).astype(jnp.bfloat16)
    outgoing = outgoing.reshape(n_experts, most, width)
    arrived = lax.all_to_all(outgoing, EXPERT, split_axis=0, concat_axis=0, tiled=True).reshape(
        slots_all, width
    )
    pieces = gather_turned((w_gate, w_up, w_down), "dp", (2, 2, 2))
    produced = expert_rows(arrived, pieces[0][0], pieces[1][0], pieces[2][0])
    answer = produced.astype(jnp.bfloat16).reshape(n_experts, most, width)
    back = lax.all_to_all(answer, EXPERT, split_axis=0, concat_axis=0, tiled=True).reshape(
        slots_all, width
    )
    picked = back[send_slot].astype(jnp.float32) * weight[:, None]
    mixed = jnp.sum(picked.reshape(tok_rows, 2, width), axis=1)
    return mixed.astype(jnp.bfloat16)


def solution(mesh):
    finer = Mesh(
        mesh.devices.reshape(mesh.shape["dp"], 8, 4, 2), ("dp", "expert_0", "expert_1", "expert_2")
    )
    return jax.shard_map(
        local,
        mesh=finer,
        in_specs=(
            P(DP_EXPERT, None),
            P(DP_EXPERT, None),
            P(DP_EXPERT, None),
            P(),
            P(EXPERT, None, "dp"),
            P(EXPERT, None, "dp"),
            P(EXPERT, None, "dp"),
        ),
        out_specs=P(DP_EXPERT, None),
        check_vma=False,
    )
```

profile of v0, /device:TPU:1, one launch (start us, length us, event | category | flops | bytes accessed | tf_op | source)
XLA Modules:
  0.0 272.1 jit_solution(670092717847320149)
XLA Ops:
  6.5 3.8 %pad_maximum_fusion = bf16[352,6144]{1,0:T(8,128)(2,1)} fusion(bf16[352,2048]{1,0:T(8,128)(2,1)} %bitcast.106, bf16[352,2048]{1,0:T(8,128)(2,1)} %bitcast.107, bf16[352,2048]{1,0:T(8,128)(2,1)} %bitcast.108), kind=kLoop, calls=%fused_computation.7 | loop fusion | flops 12976128 | bytes 8650752 | tf_op jit(solution)/shard_map/concatenate | solution.py:32
  10.5 0.6 copy-done.1
  11.2 0.1 eq.39
  11.3 0.1 eq.43
  11.5 0.6 dynamic-slice.1
  12.1 0.7 dynamic-slice
  14.1 0.6 reduce-window.6
  14.7 0.2 slice_reduce_fusion
  15.1 0.2 dynamic-update-slice
  15.3 4.7 %all-reduce = s32[128]{0:T(128)S(1)} all-reduce(s32[128]{0:T(128)S(1)} %dynamic-update-slice), channel_id=2, replica_groups=mesh['dp'=4,'expert_0'=8,'expert_1'=4,'expert_2'=2] {'expert_2'}, use_global_device_ids=true, to_apply=%add | all-reduce | flops 128 | bytes 1024
  20.0 0.2 fusion.26
  20.1 5.3 %all-reduce.1 = s32[256]{0:T(256)S(1)} all-reduce(s32[256]{0:T(256)S(1)} %fusion.26), channel_id=3, replica_groups=mesh['dp'=4,'expert_0'=8,'expert_1'=4,'expert_2'=2] {'expert_1'}, use_global_device_ids=true, to_apply=%add.1 | all-reduce | flops 256 | bytes 2048
  25.5 15.8 %all-gather.2 = s32[8,1,64]{2,1,0:T(1,128)S(1)} all-gather(s32[1,1,64]{2,1,0:T(1,128)S(1)} %fusion.32), channel_id=1, replica_groups=mesh['dp'=4,'expert_0'=8,'expert_1'=4,'expert_2'=2] {'expert_0'}, dimensions={0}, use_global_device_ids=true | all-gather | bytes 2304 | tf_op jit(solution)/shard_map/all_gather | solution.py:20
  41.3 9.6 %all-gather.3 = s32[4,1,64]{2,1,0:T(1,128)S(1)} all-gather(s32[1,1,64]{2,1,0:T(1,128)S(1)} %bitcast.110), channel_id=1, replica_groups=mesh['dp'=4,'expert_0'=8,'expert_1'=4,'expert_2'=2] {'dp'}, dimensions={0}, use_global_device_ids=true | all-gather | bytes 1280 | tf_op jit(solution)/shard_map/all_gather | solution.py:20
  51.1 0.1 reduce_sum.63
  51.4 0.2 reduce_sum.68
  51.6 0.2 reduce_sum.66
  51.9 1.6 convolution_convert_fusion
  53.5 2.4 reshape.138
  55.9 60.4 %all_to_all.10 = bf16[64,5,2048]{2,1,0:T(8,128)(2,1)} all-to-all(bf16[64,5,2048]{2,1,0:T(8,128)(2,1)S(1)} %reshape.138), channel_id=1, replica_groups=mesh['dp'=4,'expert_0'=8,'expert_1'=4,'expert_2'=2] {'expert_0','expert_..., dimensions={0} | all-to-all | bytes 2621440 | tf_op jit(solution)/shard_map/all_to_all | solution.py:76
  116.3 2.6 reshape.139
  118.9 57.4 %all-gather.6.cloned.1.call-done = bf16[1408,6144]{1,0:T(8,128)(2,1)} async-done(((bf16[352,6144]{1,0:T(8,128)(2,1)}), bf16[1408,6144]{1,0:T(8,128)(2,1)}) %all-gather.6.cloned.1.call-update) | async-done | bytes 17301520 | tf_op jit(solution)/shard_map/all_gather | solution.py:33
  176.3 6.1 %fusion.2 = f32[320,1408]{1,0:T(8,128)} fusion(bf16[320,2048]{1,0:T(8,128)(2,1)S(1)} %reshape.139, bf16[1408,6144]{1,0:T(8,128)(2,1)} %all-gather.6.cloned.1.call-done), kind=kOutput, calls=%fused_computation.6 | convolution fusion | flops 1845493760 | bytes 8880128 | tf_op jit(solution)/shard_map/dot_general | solution.py:42
  182.4 9.2 %fusion.4 = bf16[320,2048]{1,0:T(8,128)(2,1)S(1)} fusion(bf16[1408,6144]{1,0:T(8,128)(2,1)} %all-gather.6.cloned.1.call-done, bf16[320,2048]{1,0:T(8,128)(2,1)S(1)} %reshape.139, f32[320,1408]{1,0:T(8,128)} %fusion.2), kind=kOutput, calls=%fused_computation.9 | convolution fusion | flops 3694346240 | bytes 15958016 | tf_op jit(solution)/shard_map/dot_general | solution.py:45
  191.7 1.6 reshape.146
  193.2 11.1 %all-to-all-start.1 = ((bf16[64,5,2048]{2,1,0:T(8,128)(2,1)}), bf16[64,5,2048]{2,1,0:T(8,128)(2,1)}, u32[]{:S(2)}, u32[]{:S(2)}) async-start(bf16[64,5,2048]{2,1,0:T(8,128)(2,1)} %reshape.146), calls=%async_computation.1 | async-start | bytes 4194304 | tf_op jit(solution)/shard_map/all_to_all | solution.py:82
  204.3 0.1 mul.67
  204.6 49.3 %all-to-all-done.1 = bf16[64,5,2048]{2,1,0:T(8,128)(2,1)} async-done(((bf16[64,5,2048]{2,1,0:T(8,128)(2,1)}), bf16[64,5,2048]{2,1,0:T(8,128)(2,1)}, u32[]{:S(2)}, u32[]{:S(2)}) %all-to-all-start.1) | async-done | bytes 1310752 | tf_op jit(solution)/shard_map/all_to_all | solution.py:82
  253.9 2.6 reshape.147
  256.5 2.3 gather_fusion
  258.8 2.4 reshape.148
  261.2 4.0 %multiply_reduce_fusion = bf16[128,2048]{1,0:T(8,128)(2,1)} fusion(f32[128,2,2048]{2,1,0:T(2,128)S(1)} %reshape.148, f32[128,2]{1,0:T(8,128)S(1)} %copy.39), kind=kLoop, calls=%fused_computation.12 | loop fusion | flops 786432 | bytes 2622464 | tf_op jit(solution)/shard_map/reduce_sum | solution.py:86
  (34 shorter events, 1.1 us)
Async XLA Ops:
  6.5 45.4 %copy-start = (bf16[128,2048]{1,0:T(8,128)(2,1)S(1)}, bf16[128,2048]{1,0:T(8,128)(2,1)}, u32[]{:S(2)}) copy-start(bf16[128,2048]{1,0:T(8,128)(2,1)} %param.7) | copy-start | bytes 1572868
  6.5 169.8 %all-gather.6.cloned.1.call-start = ((), (), s32[]{:S(2)}) async-start(), calls=%async_computation.2 | async-start | bytes 21626880 | tf_op jit(solution)/shard_map/all_gather | solution.py:33
  10.4 0.7 copy-start.1
  10.4 1.1 copy-start.5
  10.4 1.7 copy-start.4
  10.4 40.6 %copy-start.3 = (s32[64]{0:T(128)S(1)}, s32[64]{0:T(128)}, u32[]{:S(2)}) copy-start(s32[64]{0:T(128)} %param.10) | copy-start | bytes 772
  10.4 41.4 %copy-start.2 = (s32[128,2]{0,1:T(2,128)S(1)}, s32[128,2]{0,1:T(2,128)}, u32[]{:S(2)}) copy-start(s32[128,2]{0,1:T(2,128)} %param.9) | copy-start | bytes 3076
  193.2 60.7 %all-to-all-start.1 = ((bf16[64,5,2048]{2,1,0:T(8,128)(2,1)}), bf16[64,5,2048]{2,1,0:T(8,128)(2,1)}, u32[]{:S(2)}, u32[]{:S(2)}) async-start(bf16[64,5,2048]{2,1,0:T(8,128)(2,1)} %reshape.146), calls=%async_computation.1 | async-start | bytes 4194304 | tf_op jit(solution)/shard_map/all_to_all | solution.py:82
Sparse Core Ops, SparseCore 0:
  10.6 165.7 all-gather.5
where the time goes:
time: 273 us; the launch traced here: 272 us
  waiting for transfers between devices  107 us (39%)
  blocking collectives  95.8 us (35%)
  local copies, waits for them, and re-layouts  17.4 us (6%)
  matrix products  16.9 us (6%)
  between operations  15 us (5%)
  starting transfers between devices  11.1 us (4%)
  other arithmetic  9.2 us (3%)
    all_to_all x1, blocking collectives, local(): lax.all_to_all(outgoing, EXPERT, split_axis=0, concat_axis=0, tiled=True)  60.4 us
    all_gather x1, waiting for transfers between devices, gather_turned(): lax.all_gather(both, axis, axis=0, tiled=True)  57.4 us
    all_to_all x1, waiting for transfers between devices, local(): lax.all_to_all(answer, EXPERT, split_axis=0, concat_axis=0, tiled=True)  49.3 us
    all_gather x2, blocking collectives, carried_in(): pieces = lax.all_gather(total, axis)  25.3 us
    all_to_all x1, starting transfers between devices, local(): lax.all_to_all(answer, EXPERT, split_axis=0, concat_axis=0, tiled=True)  11.1 us
    unnamed x2, blocking collectives  9.99 us
    dot_general x1, matrix products, expert_rows(): lax.dot_general(hidden, down_w, (((1,), (1,)), ((), ())), preferred_eleme...  9.2 us
    dot_general x1, matrix products, expert_rows(): gate = jnp.dot(rows, gate_w, preferred_element_type=jnp.float32)  6.1 us
  transfers between devices with their start and end apart: 2, of which 2 were waited for; matrix products, arithmetic and copies ran while one was open for 4% of the time, Pallas kernels for 0%

commit v1 on v0

v1 whole, which is shorter than its diff:
```python
import functools

import jax
import jax.numpy as jnp
from jax import lax
from jax.experimental import pallas as pl
from jax.experimental.pallas import tpu as pltpu
from jax.sharding import Mesh
from jax.sharding import PartitionSpec as P

MESH = pl.DeviceIdType.MESH
AXES = ("dp", "expert_0", "expert_1", "expert_2")
EXPERT = ("expert_0", "expert_1", "expert_2")
BF16, F32, I32 = jnp.bfloat16, jnp.float32, jnp.int32
LANES = 128
ROW_TILE = 16


def z_groups(nz):
    half = nz // 2
    pairs = [(0, 1)] + [(-k, k + 1) for k in range(1, half)]
    return pairs[:1] + pairs[2:] + pairs[1:2]


def log2(n):
    assert n & (n - 1) == 0
    return n.bit_length() - 1


def kernel(
    shape, most,
    tokens, ids, units, cap, wg_h, wu_h, wd_h, out,
    wg, wu, wd, perm, rows2d, out3, recv3, ret3, back3, a2d, hid, own, pf, part, rs1, rs2,
    sel, whi, wlo, acc, cnt_mine, cnt_all, tot_mine, tot_all,
    w_sem, a2a_send, a2a_recv, ag_send, ag_recv, rs_send, rs_recv, back_send, back_recv, cnt_send, cnt_recv, tot_send, tot_recv,
):
    nx, nz, ny, nc = shape
    x, z, y, c = (lax.axis_index(a) for a in AXES)
    right, left, opp = lax.rem(x + 1, nx), lax.rem(x + nx - 1, nx), lax.rem(x + 2, nx)
    plane = nz * ny * nc
    per_z = ny * nc
    groups = z_groups(nz)
    per_group = 2 * per_z
    gr = per_group * most
    blocks = gr // ROW_TILE
    t_rows, width = tokens.shape
    half = width // 2
    lo, hi = pl.ds(0, half), pl.ds(half, half)

    def at_x(new_x):
        return (new_x, z, y, c)

    def relative(sign, dz, dy, dc):
        return (
            x,
            lax.rem(z + sign * dz + 2 * nz, nz),
            lax.rem(y + sign * dy + ny, ny),
            lax.rem(c + sign * dc + nc, nc),
        )

    def split(i):
        return i // per_z, lax.rem(i // nc, ny), lax.rem(i, nc)

    barrier = pltpu.get_barrier_semaphore()

    def greet(i, carry):
        pl.semaphore_signal(barrier, inc=1, device_id=relative(1, *split(i)), device_id_type=MESH)
        return carry

    for new_x in (right, left, opp):
        pl.semaphore_signal(barrier, inc=1, device_id=at_x(new_x), device_id_type=MESH)
    lax.fori_loop(1, plane, greet, 0)

    loads = [
        pltpu.make_async_copy(src.at[0], dst, w_sem.at[i])
        for i, (src, dst) in enumerate(((wg_h, wg), (wu_h, wu), (wd_h, wd)))
    ]
    for load in loads:
        load.start()

    lane = lax.broadcasted_iota(I32, (t_rows, LANES), 1)
    id0, id1 = ids[:, 0:1], ids[:, 1:2]
    oh0, oh1 = (lane == id0).astype(F32), (lane == id1).astype(F32)
    named = oh0 + oh1
    counts = jnp.sum(named, axis=0, keepdims=True)
    cnt_mine[...] = counts
    cnt_all[0] = counts
    earlier = (
        lax.broadcasted_iota(I32, (t_rows, t_rows), 1) < lax.broadcasted_iota(I32, (t_rows, t_rows), 0)
    ).astype(BF16)
    before = jnp.dot(earlier, named.astype(BF16), preferred_element_type=F32)
    rank0 = jnp.sum(before * oh0, axis=1, keepdims=True)
    rank1 = jnp.sum(before * oh1, axis=1, keepdims=True)

    def slot_of(expert, rank):
        ez = lax.shift_right_logical(expert, log2(per_z))
        ey = lax.shift_right_logical(expert, log2(nc)) & (ny - 1)
        ec = expert & (nc - 1)
        dz = (ez - z + nz) & (nz - 1)
        dy = (ey - y + ny) & (ny - 1)
        dc = (ec - c + nc) & (nc - 1)
        place = jnp.zeros_like(dz)
        for g, pair in enumerate(groups):
            for zi, off in enumerate(pair):
                place = jnp.where(dz == off % nz, 2 * g + zi, place)
        return (place * per_z + dy * nc + dc) * most + rank.astype(I32)

    pos0, pos1 = slot_of(id0, rank0), slot_of(id1, rank1)

    i_row = lax.broadcasted_iota(I32, (256, 256), 0)
    i_col = lax.broadcasted_iota(I32, (256, 256), 1)
    swapped = (i_row & 15) * 16 + lax.shift_right_logical(i_row, 4)
    perm[...] = (i_col == swapped).astype(BF16)

    def to_tiles(dst3, g):
        for b in range(blocks):
            block = rows2d[ROW_TILE * b : ROW_TILE * (b + 1), :]
            stacked = jnp.concatenate(
                [block[:, LANES * s : LANES * (s + 1)] for s in range(width // LANES)], axis=0
            )
            turned = jnp.dot(perm[...], stacked, preferred_element_type=F32).astype(BF16)
            r = g * gr + ROW_TILE * b
            dst3[r : r + ROW_TILE] = turned.reshape(ROW_TILE, ROW_TILE, LANES)

    def from_tiles(src3, g, dst):
        for b in range(blocks):
            r = g * gr + ROW_TILE * b
            stacked = src3[r : r + ROW_TILE].reshape(ROW_TILE * ROW_TILE, LANES)
            turned = jnp.dot(perm[...], stacked, preferred_element_type=F32).astype(BF16)
            for s in range(width // LANES):
                dst[ROW_TILE * b : ROW_TILE * (b + 1), LANES * s : LANES * (s + 1)] = turned[
                    ROW_TILE * s : ROW_TILE * (s + 1), :
                ]

    def exchange(src, dst, g, sign, send_sem, recv_sem):
        a, b = groups[g]
        first = 1 if a == 0 else 0
        base = g * per_group

        def one(i, carry):
            zi, dy, dc = split(i)
            rows = pl.ds((base + i) * most, most)
            pltpu.make_async_remote_copy(
                src_ref=src.at[rows],
                dst_ref=dst.at[rows],
                send_sem=send_sem.at[g],
                recv_sem=recv_sem.at[g],
                device_id=relative(sign, a + zi * (b - a), dy, dc),
                device_id_type=MESH,
            ).start()
            return carry

        lax.fori_loop(first, per_group, one, 0)
        if first:
            dst[base * most : (base + 1) * most] = src[base * most : (base + 1) * most]

    def exchanged(ref, g, sem):
        first = 1 if groups[g][0] == 0 else 0
        rows = pl.ds((g * per_group + first) * most, (per_group - first) * most)
        pltpu.make_async_copy(ref.at[rows], ref.at[rows], sem.at[g]).wait()

    slots = lax.broadcasted_iota(I32, (t_rows, gr), 1)

    def gather(g):
        s0, s1 = (slots + g * gr == pos0), (slots + g * gr == pos1)
        chosen = (s0.astype(F32) + s1.astype(F32)).astype(BF16)
        rows = lax.dot_general(
            chosen, tokens[...], (((0,), (0,)), ((), ())), preferred_element_type=F32
        )
        rows2d[...] = rows.astype(BF16)
        to_tiles(out3, g)

    sent = []

    def push(src, dst, send_sem, recv_sem, new_x):
        copy = pltpu.make_async_remote_copy(
            src_ref=src, dst_ref=dst, send_sem=send_sem, recv_sem=recv_sem,
            device_id=at_x(new_x), device_id_type=MESH,
        )
        copy.start()
        sent.append(copy)

    def arrive(ref, sem):
        pltpu.make_async_copy(ref, ref, sem).wait()

    def rows_of(slot):
        return pl.ds(slot * gr, gr)

    def s1(g):
        exchanged(recv3, g, a2a_recv)
        from_tiles(recv3, g, a2d.at[g])
        me = rows_of(0)
        push(a2d.at[g, me, lo], a2d.at[g, rows_of(1), lo], ag_send.at[g, 0], ag_recv.at[g, 0], right)
        push(a2d.at[g, me, hi], a2d.at[g, rows_of(2), hi], ag_send.at[g, 1], ag_recv.at[g, 1], left)
        push(a2d.at[g, me, hi], a2d.at[g, rows_of(1), hi], ag_send.at[g, 2], ag_recv.at[g, 2], right)
        push(a2d.at[g, me, lo], a2d.at[g, rows_of(2), lo], ag_send.at[g, 3], ag_recv.at[g, 3], left)

    def s2(g):
        arrive(a2d.at[g, rows_of(1), lo], ag_recv.at[g, 0])
        push(a2d.at[g, rows_of(1), lo], a2d.at[g, rows_of(3), lo], ag_send.at[g, 4], ag_recv.at[g, 4], right)
        arrive(a2d.at[g, rows_of(2), hi], ag_recv.at[g, 1])
        push(a2d.at[g, rows_of(2), hi], a2d.at[g, rows_of(3), hi], ag_send.at[g, 5], ag_recv.at[g, 5], left)

    def s3(g):
        arrive(a2d.at[g, rows_of(1), hi], ag_recv.at[g, 2])
        arrive(a2d.at[g, rows_of(2), lo], ag_recv.at[g, 3])
        arrive(a2d.at[g, rows_of(3), lo], ag_recv.at[g, 4])
        arrive(a2d.at[g, rows_of(3), hi], ag_recv.at[g, 5])
        if g == 0:
            for load in loads:
                load.wait()
        rows = a2d[g]
        gate = jnp.dot(rows, wg[...], preferred_element_type=F32)
        up = jnp.dot(rows, wu[...], preferred_element_type=F32)
        hid[...] = (gate / (1.0 + jnp.exp(-gate)) * up).astype(BF16)
        n_cols = half // 2
        for n in range(4):
            cols = slice(n * n_cols, (n + 1) * n_cols)
            res = lax.dot_general(
                hid[...], wd[cols, :], (((1,), (1,)), ((), ())), preferred_element_type=F32
            )
            own[g, :, cols] = res[0:gr]
            to_left, to_right = res[gr : 2 * gr], res[2 * gr : 3 * gr]
            in_half = slice((n % 2) * n_cols, (n % 2 + 1) * n_cols)
            if n < 2:
                part[g, 0, :, cols] = to_left.astype(BF16)
                pf[g, 1, :, in_half] = to_right
            else:
                pf[g, 0, :, in_half] = to_left
                part[g, 1, :, cols] = to_right.astype(BF16)
            part[g, 2, :, cols] = res[3 * gr : 4 * gr].astype(BF16)
        push(part.at[g, 2, :, lo], rs1.at[g, 0], rs_send.at[g, 0], rs_recv.at[g, 0], right)
        push(part.at[g, 2, :, hi], rs1.at[g, 1], rs_send.at[g, 1], rs_recv.at[g, 1], left)
        push(part.at[g, 1, :, hi], rs2.at[g, 0, :, hi], rs_send.at[g, 2], rs_recv.at[g, 2], right)
        push(part.at[g, 0, :, lo], rs2.at[g, 1, :, lo], rs_send.at[g, 3], rs_recv.at[g, 3], left)

    def s4(g):
        arrive(rs1.at[g, 0], rs_recv.at[g, 0])
        part[g, 1, :, 0:half] = (pf[g, 1] + rs1[g, 0].astype(F32)).astype(BF16)
        push(part.at[g, 1, :, lo], rs2.at[g, 0, :, lo], rs_send.at[g, 4], rs_recv.at[g, 4], right)
        arrive(rs1.at[g, 1], rs_recv.at[g, 1])
        part[g, 0, :, half:width] = (pf[g, 0] + rs1[g, 1].astype(F32)).astype(BF16)
        push(part.at[g, 0, :, hi], rs2.at[g, 1, :, hi], rs_send.at[g, 5], rs_recv.at[g, 5], left)

    def s5(g):
        arrive(rs2.at[g, 0, :, hi], rs_recv.at[g, 2])
        arrive(rs2.at[g, 1, :, lo], rs_recv.at[g, 3])
        arrive(rs2.at[g, 0, :, lo], rs_recv.at[g, 4])
        arrive(rs2.at[g, 1, :, hi], rs_recv.at[g, 5])
        total = own[g] + rs2[g, 0].astype(F32) + rs2[g, 1].astype(F32)
        rows2d[...] = total.astype(BF16)
        to_tiles(ret3, g)
        exchange(ret3, back3, g, -1, back_send, back_recv)

    def s6(g):
        exchanged(back3, g, back_recv)
        from_tiles(back3, g, rows2d)
        rows = rows2d[...]
        res = jnp.dot(whi[g], rows, preferred_element_type=F32)
        res = res + jnp.dot(wlo[g], rows, preferred_element_type=F32)
        acc[...] = acc[...] + res

    def send_counts():
        def one(i, carry):
            pltpu.make_async_remote_copy(
                src_ref=cnt_mine, dst_ref=cnt_all.at[i], send_sem=cnt_send, recv_sem=cnt_recv,
                device_id=relative(1, *split(i)), device_id_type=MESH,
            ).start()
            return carry

        lax.fori_loop(1, plane, one, 0)

    counted = {}

    def plane_counts():
        arrive(cnt_all.at[pl.ds(1, plane - 1)], cnt_recv)
        table = cnt_all[:, 0, :]
        i = lax.broadcasted_iota(I32, (plane, 1), 0)
        sz = (z - lax.shift_right_logical(i, log2(per_z)) + nz) & (nz - 1)
        sy = (y - (lax.shift_right_logical(i, log2(nc)) & (ny - 1)) + ny) & (ny - 1)
        sc = (c - (i & (nc - 1)) + nc) & (nc - 1)
        mine = (z * ny + y) * nc + c
        first = ((sz * ny + sy) * nc + sc < mine).astype(F32)
        counted["inside"] = jnp.sum(table * first, axis=0, keepdims=True)
        tot_mine[...] = jnp.sum(table, axis=0, keepdims=True)
        for k, new_x in enumerate((right, left, opp)):
            push(tot_mine, tot_all.at[k], tot_send.at[k], tot_recv.at[k], new_x)

    def weigh():
        offset = counted["inside"]
        for k, src in enumerate((left, right, opp)):
            arrive(tot_all.at[k], tot_recv.at[k])
            offset = offset + tot_all[k] * jnp.where(src < x, 1.0, 0.0)
        n_experts = cap.shape[1]
        limit = cap[...].astype(F32)
        parts = []
        for k, (oh, rank, pos) in enumerate(((oh0, rank0, pos0), (oh1, rank1, pos1))):
            slot = jnp.sum(oh * offset, axis=1, keepdims=True) + rank
            top = jnp.sum(oh[:, :n_experts] * limit, axis=1, keepdims=True)
            unit = jnp.where(slot < top, units[:, k : k + 1], 0)
            high = unit & ~7
            parts.append((pos, high.astype(F32) / 1024.0, (unit - high).astype(F32) / 1024.0))
        for g in range(len(groups)):
            for k, (pos, high, low) in enumerate(parts):
                here = slots + g * gr == pos
                if k == 0:
                    h, l = jnp.where(here, high, 0.0), jnp.where(here, low, 0.0)
                else:
                    h, l = h + jnp.where(here, high, 0.0), l + jnp.where(here, low, 0.0)
            whi[g] = h.astype(BF16)
            wlo[g] = l.astype(BF16)
        acc[...] = jnp.zeros_like(acc)

    n = len(groups)
    gather(0)
    pl.semaphore_wait(barrier, plane - 1 + nx - 1)
    exchange(out3, recv3, 0, 1, a2a_send, a2a_recv)
    for g in range(1, n):
        gather(g)
        exchange(out3, recv3, g, 1, a2a_send, a2a_recv)
    send_counts()

    if n == 4:
        order = [
            (s1, 0), (s2, 0), (s1, 1), (s3, 0), (s2, 1), (s4, 0), (plane_counts,), (s3, 1), (s1, 2), (s5, 0), (s2, 2), (s4, 1),
            (weigh,), (s1, 3), (s3, 2), (s5, 1), (s2, 3), (s4, 2), (s3, 3), (s5, 2), (s4, 3), (s6, 0), (s6, 1), (s5, 3),
            (s6, 2), (s6, 3),
        ]
    else:
        order = [(stage, g) for stage in (s1, s2, s3, s4, s5) for g in range(n)]
        order += [(plane_counts,), (weigh,)] + [(s6, g) for g in range(n)]
    for stage, *args in order:
        stage(*args)
    out[...] = acc[...].astype(BF16)

    for copy in sent:
        copy.wait_send()
    for g in range(n):
        exchanged(out3, g, a2a_send)
        exchanged(ret3, g, back_send)
    arrive(cnt_all.at[pl.ds(1, plane - 1)], cnt_send)


def local(shape, most, tokens, expert_ids, gate_units, capacity, w_gate, w_up, w_down):
    nx, nz, ny, nc = shape
    t_rows, width = tokens.shape
    ff = w_gate.shape[2]
    plane = nz * ny * nc
    n = len(z_groups(nz))
    gr = 2 * ny * nc * most
    vmem = pl.BlockSpec(memory_space=pltpu.VMEM)
    anywhere = pl.BlockSpec(memory_space=pl.ANY)
    dma = pltpu.SemaphoreType.DMA
    tiles = pltpu.VMEM((plane * most, ROW_TILE, LANES), BF16)
    return pl.pallas_call(
        functools.partial(kernel, shape, most),
        out_shape=jax.ShapeDtypeStruct((t_rows, width), BF16),
        in_specs=[vmem, vmem, vmem, vmem, anywhere, anywhere, anywhere],
        out_specs=vmem,
        scratch_shapes=[
            pltpu.VMEM((width, ff), BF16),
            pltpu.VMEM((width, ff), BF16),
            pltpu.VMEM((width, ff), BF16),
            pltpu.VMEM((256, 256), BF16),
            pltpu.VMEM((gr, width), BF16),
            tiles, tiles, tiles, tiles,
            pltpu.VMEM((n, nx * gr, width), BF16),
            pltpu.VMEM((nx * gr, ff), BF16),
            pltpu.VMEM((n, gr, width), F32),
            pltpu.VMEM((n, 2, gr, width // 2), F32),
            pltpu.VMEM((n, 3, gr, width), BF16),
            pltpu.VMEM((n, 2, gr, width // 2), BF16),
            pltpu.VMEM((n, 2, gr, width), BF16),
            pltpu.VMEM((8, LANES), F32),
            pltpu.VMEM((n, t_rows, gr), BF16),
            pltpu.VMEM((n, t_rows, gr), BF16),
            pltpu.VMEM((t_rows, width), F32),
            pltpu.VMEM((1, LANES), F32),
            pltpu.VMEM((plane, 1, LANES), F32),
            pltpu.VMEM((1, LANES), F32),
            pltpu.VMEM((3, 1, LANES), F32),
            dma((3,)),
            dma((n,)), dma((n,)),
            dma((n, 6)), dma((n, 6)),
            dma((n, 6)), dma((n, 6)),
            dma((n,)), dma((n,)),
            dma, dma,
            dma((3,)), dma((3,)),
        ],
        compiler_params=pltpu.CompilerParams(collective_id=0, has_side_effects=True),
    )(tokens, expert_ids, gate_units, capacity.reshape(1, -1), w_gate, w_up, w_down)


def build(finer, most):
    shape = tuple(finer.shape[a] for a in AXES)
    return jax.shard_map(
        functools.partial(local, shape, most),
        mesh=finer,
        in_specs=(
            P(AXES, None),
            P(AXES, None),
            P(AXES, None),
            P(),
            P(EXPERT, None, "dp"),
            P(EXPERT, None, "dp"),
            P(EXPERT, None, "dp"),
        ),
        out_specs=P(AXES, None),
        check_vma=False,
    )


def solution(mesh):
    finer = Mesh(mesh.devices.reshape(mesh.shape["dp"], 8, 4, 2), AXES)
    return build(finer, 5)
```

time: 273 us -> 136 us (0.50)
  Pallas kernels: 0 us -> 125 us
  waiting for transfers between devices: 107 us -> 0 us
  blocking collectives: 95.8 us -> 0 us
  matrix products: 16.9 us -> 0 us
  between operations: 15 us -> 0.01 us
  starting transfers between devices: 11.1 us -> 0 us
  other arithmetic: 9.2 us -> 0 us
  local copies, waits for them, and re-layouts: 17.4 us -> 10.5 us
    pallas_call x0 -> x1, Pallas kernels: none -> 125 us  [local(): pl.pallas_call(functools.partial(kernel, shape, most), out_shape=jax.Shap...]
    all_to_all x1 -> x0, blocking collectives: 60.4 us -> none  [local(): lax.all_to_all(outgoing, EXPERT, split_axis=0, concat_axis=0, tiled=True)]
    all_gather x1 -> x0, waiting for transfers between devices: 57.4 us -> none  [gather_turned(): lax.all_gather(both, axis, axis=0, tiled=True)]
    all_to_all x1 -> x0, waiting for transfers between devices: 49.3 us -> none  [local(): lax.all_to_all(answer, EXPERT, split_axis=0, concat_axis=0, tiled=True)]
    all_gather x2 -> x0, blocking collectives: 25.3 us -> none  [carried_in(): pieces = lax.all_gather(total, axis)]
    dot_general x3 -> x0, matrix products: 16.9 us -> none  [the longest x1 9.2 us: expert_rows(): lax.dot_general(hidden, down_w, (((1,), (1,)), ((), ())), preferred_eleme...]
    all_to_all x1 -> x0, starting transfers between devices: 11.1 us -> none  [local(): lax.all_to_all(answer, EXPERT, split_axis=0, concat_axis=0, tiled=True)]
    unnamed x2 -> x0, blocking collectives: 9.99 us -> none
  transfers between devices with their start and end apart: 2 -> 0, of which waited for: 2 -> 0; matrix products, arithmetic and copies ran while one was open for 4% -> 0% of each run, Pallas kernels for 0% -> 0%
where the time goes in v1:
time: 136 us
  Pallas kernels  125 us (92%)
  local copies, waits for them, and re-layouts  10.5 us (8%)
    pallas_call x1, Pallas kernels, local(): pl.pallas_call(functools.partial(kernel, shape, most), out_shape=jax.Shap...  125 us
    unnamed x10, local copies, waits for them, and re-layouts  10.5 us

profile of v1, /device:TPU:1, one launch (start us, length us, event | category | flops | bytes accessed | tf_op | source)
XLA Modules:
  0.0 135.6 jit_solution(12066108682216531970)
XLA Ops:
  0.0 0.0 copy-start
  0.0 1.5 %copy.8.ids = s32[128,2]{1,0:T(8,128)} copy(s32[128,2]{0,1:T(2,128)} %param.8) | data formatting | bytes 2048 | tf_op args[1]
  1.5 1.4 %copy.9.units = s32[128,2]{1,0:T(8,128)} copy(s32[128,2]{0,1:T(2,128)} %param.9) | data formatting | bytes 2048 | tf_op args[2]
  2.9 2.6 %copy.10.wg_h = bf16[1,2048,352]{2,1,0:T(8,128)(2,1)} copy(bf16[1,2048,352]{1,2,0:T(8,128)(2,1)} %param.11) | data formatting | bytes 2883584 | tf_op args[4]
  5.5 0.0 copy-done
  5.5 0.0 copy-start.1
  5.5 1.6 %copy.11.wu_h = bf16[1,2048,352]{2,1,0:T(8,128)(2,1)} copy(bf16[1,2048,352]{1,2,0:T(8,128)(2,1)S(1)} %copy-done) | data formatting | bytes 2883584 | tf_op args[5]
  7.1 0.0 copy-done.1
  7.1 1.6 %copy.12.wd_h = bf16[1,2048,352]{2,1,0:T(8,128)(2,1)} copy(bf16[1,2048,352]{1,2,0:T(8,128)(2,1)S(1)} %copy-done.1) | data formatting | bytes 2883584 | tf_op args[6]
  8.6 125.0 %shard_map.73 = bf16[128,2048]{1,0:T(8,128)(2,1)} custom-call(bf16[128,2048]{1,0:T(8,128)(2,1)} %tokens.1, s32[128,2]{1,0:T(8,128)} %copy.8.ids, s32[128,2]{1,0:T(8,128)} %copy.9.units, s32[1,64]{1,0:T(1,128)} %bitcast.1, bf16[1,2048,352]{2,1,0:T(8,128)(2,1)} %copy.10.wg_h, bf16[1,2048,352]{2,1,0:T(8,128)(2,1)} %copy.11.wu_h, bf16[1,2048,352]{2,1,0:T(8,128)(2,1)} %copy.12.wd_h), custom_call_target="tpu_custom_call" | custom-call | tf_op jit(solution)/shard_map/pallas_call | solution.py:355
  133.7 1.9 %copy.14 = bf16[128,2048]{1,0:T(8,128)(2,1)} copy(bf16[128,2048]{1,0:T(8,128)(2,1)} %shard_map.73) | data formatting | bytes 1048576
Async XLA Ops:
  0.0 5.5 %copy-start = (bf16[1,2048,352]{1,2,0:T(8,128)(2,1)S(1)}, bf16[1,2048,352]{1,2,0:T(8,128)(2,1)}, u32[]{:S(2)}) copy-start(bf16[1,2048,352]{1,2,0:T(8,128)(2,1)} %param.12) | copy-start | bytes 4325380
  5.5 1.6 %copy-start.1 = (bf16[1,2048,352]{1,2,0:T(8,128)(2,1)S(1)}, bf16[1,2048,352]{1,2,0:T(8,128)(2,1)}, u32[]{:S(2)}) copy-start(bf16[1,2048,352]{1,2,0:T(8,128)(2,1)} %param.13) | copy-start | bytes 4325380

commit v2 on v1

--- a/solution.py
+++ b/solution.py
@@ -16,10 +16,18 @@
 ROW_TILE = 16
 
 
-def z_groups(nz):
-    half = nz // 2
-    pairs = [(0, 1)] + [(-k, k + 1) for k in range(1, half)]
-    return pairs[:1] + pairs[2:] + pairs[1:2]
+def offset_groups(nz, ny):
+    if (nz, ny) != (8, 4):
+        first = [(dz, dy) for dz in (0, 1) for dy in range(ny)]
+        return [first] + [
+            [(dz, dy) for dz in (-k, k + 1) for dy in range(ny)] for k in reversed(range(1, nz // 2))
+        ]
+    return [
+        [(0, 0), (0, 1), (0, 2), (0, 3), (1, 0), (-1, 0), (1, 3), (-1, 3)],
+        [(-2, 2), (-2, 3), (3, 0), (3, 1), (-3, 0), (-3, 1), (4, 0), (4, 1)],
+        [(2, 2), (2, 3), (3, 2), (3, 3), (-3, 2), (-3, 3), (4, 2), (4, 3)],
+        [(1, 1), (-1, 1), (1, 2), (-1, 2), (2, 0), (-2, 0), (2, 1), (-2, 1)],
+    ]
 
 
 def log2(n):
@@ -29,18 +37,18 @@
 
 def kernel(
     shape, most,
-    tokens, ids, units, cap, wg_h, wu_h, wd_h, out,
-    wg, wu, wd, perm, rows2d, out3, recv3, ret3, back3, a2d, hid, own, pf, part, rs1, rs2,
+    tokens_h, ids_h, units_h, cap_h, wg_h, wu_h, wd_h, out,
+    tokens, ids, units, cap, wg, wu, wd, perm, rows2d, out3, recv3, ret3, back3, a2d, hid, own, pf, part, rs1, rs2,
     sel, whi, wlo, acc, cnt_mine, cnt_all, tot_mine, tot_all,
-    w_sem, a2a_send, a2a_recv, ag_send, ag_recv, rs_send, rs_recv, back_send, back_recv, cnt_send, cnt_recv, tot_send, tot_recv,
+    near, w_sem, a2a_send, a2a_recv, ag_send, ag_recv, rs_send, rs_recv, back_send, back_recv, cnt_send, cnt_recv, tot_send, tot_recv,
 ):
     nx, nz, ny, nc = shape
     x, z, y, c = (lax.axis_index(a) for a in AXES)
     right, left, opp = lax.rem(x + 1, nx), lax.rem(x + nx - 1, nx), lax.rem(x + 2, nx)
     plane = nz * ny * nc
     per_z = ny * nc
-    groups = z_groups(nz)
-    per_group = 2 * per_z
+    groups = offset_groups(nz, ny)
+    per_group = len(groups[0]) * nc
     gr = per_group * most
     blocks = gr // ROW_TILE
     t_rows, width = tokens.shape
@@ -62,35 +70,61 @@
         return i // per_z, lax.rem(i // nc, ny), lax.rem(i, nc)
 
     barrier = pltpu.get_barrier_semaphore()
+    nearby = min(3, nz) * per_z
 
     def greet(i, carry):
-        pl.semaphore_signal(barrier, inc=1, device_id=relative(1, *split(i)), device_id_type=MESH)
+        dz, dy, dc = split(i)
+        dz = jnp.where(dz == 2, -1, dz)
+        pl.semaphore_signal(barrier, inc=1, device_id=relative(1, dz, dy, dc), device_id_type=MESH)
         return carry
 
     for new_x in (right, left, opp):
         pl.semaphore_signal(barrier, inc=1, device_id=at_x(new_x), device_id_type=MESH)
-    lax.fori_loop(1, plane, greet, 0)
-
+    lax.fori_loop(1, nearby, greet, 0)
+
+    small = [
+        pltpu.make_async_copy(src, dst, w_sem.at[i])
+        for i, (src, dst) in enumerate(((ids_h, ids), (tokens_h, tokens), (units_h, units), (cap_h, cap)))
+    ]
     loads = [
-        pltpu.make_async_copy(src.at[0], dst, w_sem.at[i])
+        pltpu.make_async_copy(src.at[0], dst, w_sem.at[4 + i])
         for i, (src, dst) in enumerate(((wg_h, wg), (wu_h, wu), (wd_h, wd)))
     ]
-    for load in loads:
+    for load in small + loads:
         load.start()
 
-    lane = lax.broadcasted_iota(I32, (t_rows, LANES), 1)
-    id0, id1 = ids[:, 0:1], ids[:, 1:2]
-    oh0, oh1 = (lane == id0).astype(F32), (lane == id1).astype(F32)
-    named = oh0 + oh1
-    counts = jnp.sum(named, axis=0, keepdims=True)
-    cnt_mine[...] = counts
-    cnt_all[0] = counts
+    def near_ready():
+        pl.semaphore_wait(barrier, nearby - 1 + nx - 1)
+
+    def tell(step):
+        for dz in (1, -1):
+            pl.semaphore_signal(near.at[step], inc=1, device_id=relative(1, dz, 0, 0), device_id_type=MESH)
+
+    def told(step):
+        pl.semaphore_wait(near.at[step], 2)
+
+    i_row = lax.broadcasted_iota(I32, (256, 256), 0)
+    i_col = lax.broadcasted_iota(I32, (256, 256), 1)
+    swapped = (i_row & 15) * 16 + lax.shift_right_logical(i_row, 4)
+    perm[...] = (i_col == swapped).astype(BF16)
+    small[0].wait()
+
+    n_experts = cap.shape[1]
+    expert = lax.broadcasted_iota(I32, (n_experts, t_rows), 0)
+    id0, id1 = ids[0:1, :], ids[1:2, :]
+    oh0, oh1 = (expert == id0).astype(F32), (expert == id1).astype(F32)
+    named = (oh0 + oh1).astype(BF16)
+    counts = lax.dot_general(
+        jnp.ones((8, t_rows), BF16), named, (((1,), (1,)), ((), ())), preferred_element_type=F32
+    )[0:1, :]
+    cnt_mine[:, 0:n_experts] = counts
+    cnt_all[0, :, 0:n_experts] = counts
     earlier = (
-        lax.broadcasted_iota(I32, (t_rows, t_rows), 1) < lax.broadcasted_iota(I32, (t_rows, t_rows), 0)
+        lax.broadcasted_iota(I32, (t_rows, t_rows), 0) < lax.broadcasted_iota(I32, (t_rows, t_rows), 1)
     ).astype(BF16)
-    before = jnp.dot(earlier, named.astype(BF16), preferred_element_type=F32)
-    rank0 = jnp.sum(before * oh0, axis=1, keepdims=True)
-    rank1 = jnp.sum(before * oh1, axis=1, keepdims=True)
+    before = jnp.dot(named, earlier, preferred_element_type=F32)
+    rank0 = jnp.sum(before * oh0, axis=0, keepdims=True)
+    rank1 = jnp.sum(before * oh1, axis=0, keepdims=True)
 
     def slot_of(expert, rank):
         ez = lax.shift_right_logical(expert, log2(per_z))
@@ -99,18 +133,13 @@
         dz = (ez - z + nz) & (nz - 1)
         dy = (ey - y + ny) & (ny - 1)
         dc = (ec - c + nc) & (nc - 1)
-        place = jnp.zeros_like(dz)
-        for g, pair in enumerate(groups):
-            for zi, off in enumerate(pair):
-                place = jnp.where(dz == off % nz, 2 * g + zi, place)
-        return (place * per_z + dy * nc + dc) * most + rank.astype(I32)
+        key, place = dz * ny + dy, jnp.zeros_like(dz)
+        for i, (z_off, y_off) in enumerate(pair for group in groups for pair in group):
+            place = jnp.where(key == (z_off % nz) * ny + y_off, i, place)
+        return (place * nc + dc) * most + rank.astype(I32)
 
     pos0, pos1 = slot_of(id0, rank0), slot_of(id1, rank1)
-
-    i_row = lax.broadcasted_iota(I32, (256, 256), 0)
-    i_col = lax.broadcasted_iota(I32, (256, 256), 1)
-    swapped = (i_row & 15) * 16 + lax.shift_right_logical(i_row, 4)
-    perm[...] = (i_col == swapped).astype(BF16)
+    small[1].wait()
 
     def to_tiles(dst3, g):
         for b in range(blocks):
@@ -133,40 +162,36 @@
                 ]
 
     def exchange(src, dst, g, sign, send_sem, recv_sem):
-        a, b = groups[g]
-        first = 1 if a == 0 else 0
         base = g * per_group
-
-        def one(i, carry):
-            zi, dy, dc = split(i)
-            rows = pl.ds((base + i) * most, most)
-            pltpu.make_async_remote_copy(
-                src_ref=src.at[rows],
-                dst_ref=dst.at[rows],
-                send_sem=send_sem.at[g],
-                recv_sem=recv_sem.at[g],
-                device_id=relative(sign, a + zi * (b - a), dy, dc),
-                device_id_type=MESH,
-            ).start()
-            return carry
-
-        lax.fori_loop(first, per_group, one, 0)
-        if first:
+        for i, (dz, dy) in enumerate(groups[g]):
+            for dc in range(nc):
+                rows = pl.ds((base + i * nc + dc) * most, most)
+                if dz == dy == dc == 0:
+                    assert i == 0
+                    continue
+                pltpu.make_async_remote_copy(
+                    src_ref=src.at[rows],
+                    dst_ref=dst.at[rows],
+                    send_sem=send_sem.at[g],
+                    recv_sem=recv_sem.at[g],
+                    device_id=relative(1, sign * dz, sign * dy, sign * dc),
+                    device_id_type=MESH,
+                ).start()
+        if groups[g][0] == (0, 0):
             dst[base * most : (base + 1) * most] = src[base * most : (base + 1) * most]
 
     def exchanged(ref, g, sem):
-        first = 1 if groups[g][0] == 0 else 0
+        first = 1 if groups[g][0] == (0, 0) else 0
         rows = pl.ds((g * per_group + first) * most, (per_group - first) * most)
-        pltpu.make_async_copy(ref.at[rows], ref.at[rows], sem.at[g]).wait()
-
-    slots = lax.broadcasted_iota(I32, (t_rows, gr), 1)
+        with jax.named_scope("wait"):
+            pltpu.make_async_copy(ref.at[rows], ref.at[rows], sem.at[g]).wait()
+
+    slots = lax.broadcasted_iota(I32, (gr, t_rows), 0)
 
     def gather(g):
         s0, s1 = (slots + g * gr == pos0), (slots + g * gr == pos1)
         chosen = (s0.astype(F32) + s1.astype(F32)).astype(BF16)
-        rows = lax.dot_general(
-            chosen, tokens[...], (((0,), (0,)), ((), ())), preferred_element_type=F32
-        )
+        rows = jnp.dot(chosen, tokens[...], preferred_element_type=F32)
         rows2d[...] = rows.astype(BF16)
         to_tiles(out3, g)
 
@@ -181,7 +206,8 @@
         sent.append(copy)
 
     def arrive(ref, sem):
-        pltpu.make_async_copy(ref, ref, sem).wait()
+        with jax.named_scope("wait"):
+            pltpu.make_async_copy(ref, ref, sem).wait()
 
     def rows_of(slot):
         return pl.ds(slot * gr, gr)
@@ -206,19 +232,17 @@
         arrive(a2d.at[g, rows_of(2), lo], ag_recv.at[g, 3])
         arrive(a2d.at[g, rows_of(3), lo], ag_recv.at[g, 4])
         arrive(a2d.at[g, rows_of(3), hi], ag_recv.at[g, 5])
-        if g == 0:
-            for load in loads:
-                load.wait()
+        while loads:
+            loads.pop().wait()
         rows = a2d[g]
-        gate = jnp.dot(rows, wg[...], preferred_element_type=F32)
-        up = jnp.dot(rows, wu[...], preferred_element_type=F32)
+        by_unit = (((1,), (1,)), ((), ()))
+        gate = lax.dot_general(rows, wg[...], by_unit, preferred_element_type=F32)
+        up = lax.dot_general(rows, wu[...], by_unit, preferred_element_type=F32)
         hid[...] = (gate / (1.0 + jnp.exp(-gate)) * up).astype(BF16)
         n_cols = half // 2
         for n in range(4):
             cols = slice(n * n_cols, (n + 1) * n_cols)
-            res = lax.dot_general(
-                hid[...], wd[cols, :], (((1,), (1,)), ((), ())), preferred_element_type=F32
-            )
+            res = jnp.dot(hid[...], wd[:, cols], preferred_element_type=F32)
             own[g, :, cols] = res[0:gr]
             to_left, to_right = res[gr : 2 * gr], res[2 * gr : 3 * gr]
             in_half = slice((n % 2) * n_cols, (n % 2 + 1) * n_cols)
@@ -274,7 +298,7 @@
 
     def plane_counts():
         arrive(cnt_all.at[pl.ds(1, plane - 1)], cnt_recv)
-        table = cnt_all[:, 0, :]
+        table = cnt_all[:, 0, 0:n_experts]
         i = lax.broadcasted_iota(I32, (plane, 1), 0)
         sz = (z - lax.shift_right_logical(i, log2(per_z)) + nz) & (nz - 1)
         sy = (y - (lax.shift_right_logical(i, log2(nc)) & (ny - 1)) + ny) & (ny - 1)
@@ -282,55 +306,79 @@
         mine = (z * ny + y) * nc + c
         first = ((sz * ny + sy) * nc + sc < mine).astype(F32)
         counted["inside"] = jnp.sum(table * first, axis=0, keepdims=True)
-        tot_mine[...] = jnp.sum(table, axis=0, keepdims=True)
+        tot_mine[:, 0:n_experts] = jnp.sum(table, axis=0, keepdims=True)
         for k, new_x in enumerate((right, left, opp)):
             push(tot_mine, tot_all.at[k], tot_send.at[k], tot_recv.at[k], new_x)
 
     def weigh():
+        small[2].wait()
+        small[3].wait()
         offset = counted["inside"]
         for k, src in enumerate((left, right, opp)):
             arrive(tot_all.at[k], tot_recv.at[k])
-            offset = offset + tot_all[k] * jnp.where(src < x, 1.0, 0.0)
-        n_experts = cap.shape[1]
-        limit = cap[...].astype(F32)
+            offset = offset + tot_all[k][:, 0:n_experts] * jnp.where(src < x, 1.0, 0.0)
+        diagonal = lax.broadcasted_iota(I32, (n_experts, n_experts), 0) == lax.broadcasted_iota(
+            I32, (n_experts, n_experts), 1
+        )
+
+        def down(row):
+            return jnp.sum(jnp.where(diagonal, row, 0.0), axis=1, keepdims=True)
+
+        offset, limit = down(offset), down(cap[...].astype(F32))
         parts = []
         for k, (oh, rank, pos) in enumerate(((oh0, rank0, pos0), (oh1, rank1, pos1))):
-            slot = jnp.sum(oh * offset, axis=1, keepdims=True) + rank
-            top = jnp.sum(oh[:, :n_experts] * limit, axis=1, keepdims=True)
-            unit = jnp.where(slot < top, units[:, k : k + 1], 0)
+            slot = jnp.sum(oh * offset, axis=0, keepdims=True) + rank
+            top = jnp.sum(oh * limit, axis=0, keepdims=True)
+            unit = jnp.where(slot < top, units[k : k + 1, :], 0)
             high = unit & ~7
             parts.append((pos, high.astype(F32) / 1024.0, (unit - high).astype(F32) / 1024.0))
+        wide = lax.broadcasted_iota(I32, (LANES, t_rows), 0)
         for g in range(len(groups)):
-            for k, (pos, high, low) in enumerate(parts):
-                here = slots + g * gr == pos
-                if k == 0:
-                    h, l = jnp.where(here, high, 0.0), jnp.where(here, low, 0.0)
-                else:
-                    h, l = h + jnp.where(here, high, 0.0), l + jnp.where(here, low, 0.0)
-            whi[g] = h.astype(BF16)
-            wlo[g] = l.astype(BF16)
+            h = l = jnp.zeros((LANES, t_rows), F32)
+            for pos, high, low in parts:
+                here = wide + g * gr == pos
+                h, l = h + jnp.where(here, high, 0.0), l + jnp.where(here, low, 0.0)
+            whi[g] = jnp.transpose(h)[:, 0:gr].astype(BF16)
+            wlo[g] = jnp.transpose(l)[:, 0:gr].astype(BF16)
         acc[...] = jnp.zeros_like(acc)
 
     n = len(groups)
-    gather(0)
-    pl.semaphore_wait(barrier, plane - 1 + nx - 1)
-    exchange(out3, recv3, 0, 1, a2a_send, a2a_recv)
-    for g in range(1, n):
-        gather(g)
-        exchange(out3, recv3, g, 1, a2a_send, a2a_recv)
-    send_counts()
+    issue = [0, 3, 1, 2] if n == 4 else list(range(n))
+    with jax.named_scope("gather_0"):
+        gather(0)
+    with jax.named_scope("barrier"):
+        near_ready()
+        tell(0)
+    with jax.named_scope("send_0"):
+        exchange(out3, recv3, 0, 1, a2a_send, a2a_recv)
+    steps = nz // 2 - 1
+    for step in range(steps):
+        with jax.named_scope("told"):
+            told(step)
+            if step + 1 < steps:
+                tell(step + 1)
+        if step == 0:
+            with jax.named_scope("gather"):
+                gather(issue[1])
+    for g in issue[1:]:
+        if g != issue[1]:
+            with jax.named_scope("gather"):
+                gather(g)
+        with jax.named_scope("send"):
+            exchange(out3, recv3, g, 1, a2a_send, a2a_recv)
 
     if n == 4:
         order = [
-            (s1, 0), (s2, 0), (s1, 1), (s3, 0), (s2, 1), (s4, 0), (plane_counts,), (s3, 1), (s1, 2), (s5, 0), (s2, 2), (s4, 1),
-            (weigh,), (s1, 3), (s3, 2), (s5, 1), (s2, 3), (s4, 2), (s3, 3), (s5, 2), (s4, 3), (s6, 0), (s6, 1), (s5, 3),
-            (s6, 2), (s6, 3),
+            (s1, 0), (s1, 3), (s2, 0), (s2, 3), (send_counts,), (s1, 1), (s3, 3), (s2, 1), (s1, 2), (s4, 3), (s3, 1), (s4, 1),
+            (s5, 3), (s2, 2), (plane_counts,), (s5, 1), (s3, 2), (s4, 2), (s3, 0), (weigh,), (s5, 2), (s4, 0),
+            (s6, 3), (s6, 1), (s5, 0), (s6, 2), (s6, 0),
         ]
     else:
         order = [(stage, g) for stage in (s1, s2, s3, s4, s5) for g in range(n)]
-        order += [(plane_counts,), (weigh,)] + [(s6, g) for g in range(n)]
+        order += [(send_counts,), (plane_counts,), (weigh,)] + [(s6, g) for g in range(n)]
     for stage, *args in order:
-        stage(*args)
+        with jax.named_scope("_".join([stage.__name__, *map(str, args)])):
+            stage(*args)
     out[...] = acc[...].astype(BF16)
 
     for copy in sent:
@@ -345,9 +393,10 @@
     nx, nz, ny, nc = shape
     t_rows, width = tokens.shape
     ff = w_gate.shape[2]
+    turn = functools.partial(jnp.swapaxes, axis1=-1, axis2=-2)
     plane = nz * ny * nc
-    n = len(z_groups(nz))
-    gr = 2 * ny * nc * most
+    groups = offset_groups(nz, ny)
+    n, gr = len(groups), len(groups[0]) * nc * most
     vmem = pl.BlockSpec(memory_space=pltpu.VMEM)
     anywhere = pl.BlockSpec(memory_space=pl.ANY)
     dma = pltpu.SemaphoreType.DMA
@@ -355,12 +404,16 @@
     return pl.pallas_call(
         functools.partial(kernel, shape, most),
         out_shape=jax.ShapeDtypeStruct((t_rows, width), BF16),
-        in_specs=[vmem, vmem, vmem, vmem, anywhere, anywhere, anywhere],
+        in_specs=[anywhere] * 7,
         out_specs=vmem,
         scratch_shapes=[
-            pltpu.VMEM((width, ff), BF16),
-            pltpu.VMEM((width, ff), BF16),
-            pltpu.VMEM((width, ff), BF16),
+            pltpu.VMEM((t_rows, width), BF16),
+            pltpu.VMEM((2, t_rows), I32),
+            pltpu.VMEM((2, t_rows), I32),
+            pltpu.VMEM((1, plane), I32),
+            pltpu.VMEM((ff, width), BF16),
+            pltpu.VMEM((ff, width), BF16),
+            pltpu.VMEM((ff, width), BF16),
             pltpu.VMEM((256, 256), BF16),
             pltpu.VMEM((gr, width), BF16),
             tiles, tiles, tiles, tiles,
@@ -379,7 +432,8 @@
             pltpu.VMEM((plane, 1, LANES), F32),
             pltpu.VMEM((1, LANES), F32),
             pltpu.VMEM((3, 1, LANES), F32),
-            dma((3,)),
+            pltpu.SemaphoreType.REGULAR((nz // 2 - 1,)),
+            dma((7,)),
             dma((n,)), dma((n,)),
             dma((n, 6)), dma((n, 6)),
             dma((n, 6)), dma((n, 6)),
@@ -388,7 +442,7 @@
             dma((3,)), dma((3,)),
         ],
         compiler_params=pltpu.CompilerParams(collective_id=0, has_side_effects=True),
-    )(tokens, expert_ids, gate_units, capacity.reshape(1, -1), w_gate, w_up, w_down)
+    )(tokens, turn(expert_ids), turn(gate_units), capacity.reshape(1, -1), turn(w_gate), turn(w_up), turn(w_down))
 
 
 def build(finer, most):

time: 136 us -> 122 us (0.90)
  local copies, waits for them, and re-layouts: 10.5 us -> 1.88 us
  Pallas kernels: 125 us -> 120 us
    unnamed x10 -> x1, local copies, waits for them, and re-layouts: 10.5 us -> 1.88 us
    pallas_call x1, Pallas kernels: 125 us -> 120 us  [local(): pl.pallas_call(functools.partial(kernel, shape, most), out_shape=jax.Shap...]
where the time goes in v2:
time: 122 us
  Pallas kernels  120 us (98%)
  local copies, waits for them, and re-layouts  1.88 us (2%)
    pallas_call x1, Pallas kernels, local(): pl.pallas_call(functools.partial(kernel, shape, most), out_shape=jax.Shap...  120 us

profile of v2, /device:TPU:1, one launch (start us, length us, event | category | flops | bytes accessed | tf_op | source)
XLA Modules:
  0.0 122.1 jit_solution(10582036282659237511)
XLA Ops:
  0.0 120.2 %shard_map.73 = bf16[128,2048]{1,0:T(8,128)(2,1)} custom-call(bf16[128,2048]{1,0:T(8,128)(2,1)} %tokens_h.1, s32[2,128]{1,0:T(2,128)} %bitcast.9, s32[2,128]{1,0:T(2,128)} %bitcast.10, s32[1,64]{1,0:T(1,128)} %bitcast.11, bf16[1,352,2048]{2,1,0:T(8,128)(2,1)} %bitcast.6, bf16[1,352,2048]{2,1,0:T(8,128)(2,1)} %bitcast.7, bf16[1,352,2048]{2,1,0:T(8,128)(2,1)} %bitcast.8), custom_call_target="tpu_custom_call" | custom-call | tf_op jit(solution)/shard_map/pallas_call | solution.py:404
  120.2 1.9 %copy.9 = bf16[128,2048]{1,0:T(8,128)(2,1)} copy(bf16[128,2048]{1,0:T(8,128)(2,1)} %shard_map.73) | data formatting | bytes 1048576
